TPU v7x, 32 devices: a whole 2x2x4 slice. The times are simulated.
32 devices in a mesh: turn: 4 (over y, core), blk: 4 (over z), strip: 2 (over x).
Axes of the slice: x: 2, y: 2, z: 4, core: 2. Of those that a mesh axis runs over, the one named last changes fastest.
Arguments:
- echoes: bfloat16 [2, 256, 32768], P(None, 'blk', ('turn', 'strip')), may hold values from -6 to 6
- filters: bfloat16 [2, 8, 32768], P(None, 'blk'), may hold values from -6 to 6
- slab_index: int32 [256], P(('blk', 'turn')), may hold values from 0 to 7
- shifts: int32 [256], P(('blk', 'turn')), may hold values from 0 to 32767
Outputs:
- focused: float32 [2, 256, 32768], P(None, ('blk', 'turn'), 'strip')
All inputs are finite; a program needn't handle non-finite values.
Results may differ from a plain program's by a relative error of at most 0.0003.
Values may be sent and summed in bfloat16 or wider, within the bound.
A program may use at most 128 MiB of HBM per device.

v0:
```python
import functools
import math

import jax
import jax.numpy as jnp
import numpy as np
from jax import lax
from jax.experimental import pallas as pl
from jax.experimental.pallas import tpu as pltpu
from jax.sharding import PartitionSpec as P

LANES = 128
PAIR = 2
MESH = pl.DeviceIdType.MESH
f32, bf16 = jnp.float32, jnp.bfloat16


def split_np(table):
    high = table.astype(jnp.bfloat16)
    low = (table - high.astype(np.float64)).astype(jnp.bfloat16)
    return high, low


def make_tables(length, sources, strips):
    half = LANES
    outer = length // (2 * half)
    local = outer // sources
    a_ids, c_ids = np.arange(outer), np.arange(outer)
    b_ids = np.arange(half)
    tau = np.exp(-2j * np.pi * half * c_ids / length)
    first = np.exp(-2j * np.pi * ((c_ids[:, None] * a_ids[None, :]) % outer) / outer)
    stage_one = []
    for mat in (first, tau[:, None] * first):
        grouped = mat.reshape(outer, sources, 1, local)
        top = np.concatenate([grouped.real, -grouped.imag], 2).reshape(outer, 2 * outer)
        bottom = np.concatenate([grouped.imag, grouped.real], 2).reshape(outer, 2 * outer)
        stage_one.append(np.concatenate(split_np(np.concatenate([top, bottom], 0)), 0))
    stage_one = np.stack(stage_one)
    base = np.exp(-2j * np.pi * ((b_ids[:, None] * b_ids[None, :]) % half) / half)

    def right(mat):
        whole = np.concatenate(
            [np.concatenate([mat.real, mat.imag], 1), np.concatenate([-mat.imag, mat.real], 1)], 0
        )
        high, low = split_np(whole)
        return np.concatenate([high, low, high], 0)

    stage_two = np.stack([right(base), right(base.conj())])
    twist = np.exp(-2j * np.pi * ((c_ids[:, None] * b_ids[None, :]) % length) / length)
    omega = np.exp(-2j * np.pi * b_ids / (2 * half))
    turned = twist * omega[None, :]
    twists = np.stack([twist.real, twist.imag, turned.real, turned.imag]).astype(np.float32)
    rows = outer // strips
    last = []
    for strip in range(strips):
        picked = np.arange(strip * rows, (strip + 1) * rows)
        back = np.exp(2j * np.pi * ((picked[:, None] * c_ids[None, :]) % outer) / outer) / length
        per_half = []
        for mat in (back, back * tau.conj()[None, :]):
            whole = np.concatenate(
                [np.concatenate([mat.real, -mat.imag], 1), np.concatenate([mat.imag, mat.real], 1)], 0
            )
            per_half.append(np.concatenate(split_np(whole), 0))
        last.append(np.stack(per_half))
    return stage_one, stage_two, twists, np.stack(last)


def cosine_sine(phase, length):
    quarter = length // 4
    wrapped = phase & (length - 1)
    quadrant = (wrapped + quarter // 2) // quarter if quarter & (quarter - 1) else (
        wrapped + quarter // 2
    ) >> (quarter.bit_length() - 1)
    angle = (wrapped - quadrant * quarter).astype(f32) * (2.0 * math.pi / length)
    square = angle * angle
    sine = angle * (
        1.0 + square * (-1.0 / 6 + square * (1.0 / 120 + square * (-1.0 / 5040 + square * (1.0 / 362880))))
    )
    cosine = 1.0 + square * (
        -0.5
        + square * (1.0 / 24 + square * (-1.0 / 720 + square * (1.0 / 40320 - square * (1.0 / 3628800))))
    )
    odd = (quadrant & 1) == 1
    out_cos = jnp.where(odd, sine, cosine)
    out_sin = jnp.where(odd, cosine, sine)
    quad = quadrant & 3
    out_cos = jnp.where((quad == 1) | (quad == 2), -out_cos, out_cos)
    out_sin = jnp.where(quad >= 2, -out_sin, out_sin)
    return out_cos, out_sin


def cmul(ar, ai, br, bi):
    return ar * br - ai * bi, ar * bi + ai * br


def split(values):
    high = values.astype(bf16)
    return high, (values - high.astype(f32)).astype(bf16)


def dot(left, right):
    return jnp.dot(left, right, preferred_element_type=f32)


def body(
    turns, blks, strips, length,
    shifts_ref, slabs_ref, ech_ref, filt_ref, one_ref, two_ref, twist_ref, last_ref,
    out_ref,
    recv, filt_all, inv_twist, ramp, spec,
    send_sem, recv_sem, fsend, frecv, gsend, grecv,
):
    turn, blk, strip = lax.axis_index("turn"), lax.axis_index("blk"), lax.axis_index("strip")
    row_count = recv.shape[0]
    pairs = row_count // PAIR
    slab_local = filt_ref.shape[0]
    core = lax.rem(turn, 2)
    partner = turn + 1 - 2 * core
    peers = [(dt, ds) for dt in range(turns) for ds in range(strips) if (dt, ds) != (0, 0)]

    def peer(dt, ds):
        return (lax.rem(turn + dt, turns), blk, lax.rem(strip + ds, strips))

    barrier = pltpu.get_barrier_semaphore()
    for dt, ds in peers:
        pl.semaphore_signal(barrier, inc=1, device_id=peer(dt, ds), device_id_type=MESH)
    for dz in range(1, blks):
        pl.semaphore_signal(
            barrier, inc=1, device_id=(turn, lax.rem(blk + dz, blks), strip), device_id_type=MESH
        )
    pl.semaphore_wait(barrier, len(peers) + blks - 1)

    me = turn * strips + strip

    def echo_copy(step, dt, ds):
        to = peer(dt, ds)
        return pltpu.make_async_remote_copy(
            src_ref=ech_ref.at[pl.ds(to[0] * row_count + step * PAIR, PAIR)],
            dst_ref=recv.at[pl.ds(step * PAIR, PAIR), me],
            send_sem=send_sem.at[step, dt * strips + ds],
            recv_sem=recv_sem.at[step, dt * strips + ds],
            device_id=to,
            device_id_type=MESH,
        )

    def filter_copy(dz):
        return pltpu.make_async_remote_copy(
            src_ref=filt_ref.at[:, core],
            dst_ref=filt_all.at[pl.ds(blk * slab_local, slab_local), core],
            send_sem=fsend.at[dz],
            recv_sem=frecv.at[dz],
            device_id=(turn, lax.rem(blk + dz, blks), strip),
            device_id_type=MESH,
        )

    def relay_copy(dz):
        origin = lax.rem(blk + blks - dz, blks)
        place = filt_all.at[pl.ds(origin * slab_local, slab_local), core]
        return pltpu.make_async_remote_copy(
            src_ref=place,
            dst_ref=place,
            send_sem=gsend.at[dz],
            recv_sem=grecv.at[dz],
            device_id=(partner, blk, strip),
            device_id_type=MESH,
        )

    for dz in range(1, blks):
        filter_copy(dz).start()

    def start_step(step, carry):
        for dt, ds in peers:
            echo_copy(step, dt, ds).start()
        return carry

    lax.fori_loop(0, pairs, start_step, 0)

    recv[:, me] = ech_ref[pl.ds(turn * row_count, row_count)]
    filt_all[pl.ds(blk * slab_local, slab_local)] = filt_ref[...]

    half = LANES
    outer = length // (2 * half)
    c_ids = lax.broadcasted_iota(jnp.int32, (outer, half), 0)
    lane_ids = lax.broadcasted_iota(jnp.int32, (8, 2 * half), 1)
    k_ids = jnp.where(lane_ids >= half, (lane_ids - half) * (2 * outer) + outer, lane_ids * (2 * outer))

    def prepare(row, carry):
        shift = shifts_ref[row]
        vr, vi = cosine_sine(c_ids * shift, length)
        vi = -vi
        for part in range(2):
            tr, ti = twist_ref[2 * part], -twist_ref[2 * part + 1]
            rr, ri = cmul(tr, ti, vr, vi)
            inv_twist[row, 2 * part] = rr
            inv_twist[row, 2 * part + 1] = ri
        ur, ui = cosine_sine(k_ids * shift, length)
        ramp[row, 0] = ur
        ramp[row, 1] = -ui
        return carry

    lax.fori_loop(0, row_count, prepare, 0)

    def lefts(blocks):
        highs, lows = [], []
        for re, im in blocks:
            high, low = split(jnp.concatenate([re, im], 1))
            highs.append(high)
            lows.append(low)
        high, low = jnp.concatenate(highs, 0), jnp.concatenate(lows, 0)
        return jnp.concatenate([high, high, low], 1)

    def forward(step, carry):
        for dt, ds in peers:
            echo_copy(step, dt, ds).wait_recv()
        rows = [recv[step * PAIR + i].reshape(2 * outer, 2 * half) for i in range(PAIR)]
        parts = []
        for side in range(2):
            lanes = slice(side * half, (side + 1) * half)
            res = dot(one_ref[side], jnp.concatenate([r[:, lanes] for r in rows], 1))
            parts.append(res[: 2 * outer] + res[2 * outer :])
        total, differ = parts[0] + parts[1], parts[0] - parts[1]
        blocks = []
        for e, value in enumerate((total, differ)):
            tr, ti = twist_ref[2 * e], twist_ref[2 * e + 1]
            for i in range(PAIR):
                lanes = slice(i * half, (i + 1) * half)
                blocks.append(cmul(value[:outer, lanes], value[outer:, lanes], tr, ti))
        spec[step] = dot(lefts(blocks), two_ref[0])
        return carry

    def inverse(step, carry):
        blocks = []
        for e in range(2):
            lanes = slice(e * half, (e + 1) * half)
            for i in range(PAIR):
                row = step * PAIR + i
                picked = filt_all[slabs_ref[row]].astype(f32)
                ur, ui = ramp[row, 0][:1, lanes], ramp[row, 1][:1, lanes]
                gr, gi = cmul(picked[0][:, lanes], picked[1][:, lanes], ur, ui)
                base = (e * PAIR + i) * outer
                z = spec[step, base : base + outer]
                blocks.append(cmul(z[:, :half], z[:, half:], gr, gi))
        back = dot(lefts(blocks), two_ref[1])
        lows, highs = [], []
        for i in range(PAIR):
            row = step * PAIR + i
            got = []
            for e in range(2):
                base = (e * PAIR + i) * outer
                u = back[base : base + outer]
                got.append(
                    cmul(u[:, :half], u[:, half:], inv_twist[row, 2 * e], inv_twist[row, 2 * e + 1])
                )
            lows.append(jnp.concatenate([got[0][0] + got[1][0], got[0][1] + got[1][1]], 0))
            highs.append(jnp.concatenate([got[0][0] - got[1][0], got[0][1] - got[1][1]], 0))
        rows = outer // strips
        for side, value in enumerate((lows, highs)):
            high, low = split(jnp.concatenate(value, 1))
            left = last_ref[strip, side]
            res = dot(left, high)
            res = res[: 2 * rows] + res[2 * rows :] + dot(left[: 2 * rows], low)
            for i in range(PAIR):
                row = step * PAIR + i
                for part in range(2):
                    out_ref[part, row, :, side * half : (side + 1) * half] = res[
                        part * rows : (part + 1) * rows, i * half : (i + 1) * half
                    ]
        return carry

    def both(step, carry):
        forward(step, 0)
        inverse(step, 0)
        return carry

    early = pairs // 2
    lax.fori_loop(0, early, forward, 0)
    for dz in range(1, blks):
        filter_copy(dz).wait_recv()
        relay_copy(dz).start()
    for dz in range(1, blks):
        relay_copy(dz).wait_recv()
    lax.fori_loop(0, early, inverse, 0)
    lax.fori_loop(early, pairs, both, 0)

    def end_step(step, carry):
        for dt, ds in peers:
            echo_copy(step, dt, ds).wait_send()
        return carry

    lax.fori_loop(0, pairs, end_step, 0)
    for dz in range(1, blks):
        filter_copy(dz).wait_send()
        relay_copy(dz).wait_send()


def per_device(turns, blks, strips, echoes, filters, slab_index, shifts):
    sources = turns * strips
    length = filters.shape[2]
    half = LANES
    outer = length // (2 * half)
    local = outer // sources
    row_count = slab_index.shape[0]
    slab_local = filters.shape[1]
    pairs = row_count // PAIR
    shaped = echoes.transpose(1, 0, 2).reshape(-1, 2 * local, 2 * half)
    response = (
        filters.reshape(2, slab_local, half, 2, outer)
        .transpose(1, 0, 4, 3, 2)
        .reshape(slab_local, 2, outer, 2 * half)
    )
    tables = [jnp.asarray(t) for t in make_tables(length, sources, strips)]
    vmem, smem = pl.BlockSpec(memory_space=pltpu.VMEM), pl.BlockSpec(memory_space=pltpu.SMEM)
    rows = outer // strips
    image = pl.pallas_call(
        functools.partial(body, turns, blks, strips, length),
        out_shape=jax.ShapeDtypeStruct((2, row_count, rows, 2 * half), f32),
        in_specs=[smem, smem] + [vmem] * 6,
        out_specs=vmem,
        scratch_shapes=[
            pltpu.VMEM((row_count, sources, 2 * local, 2 * half), bf16),
            pltpu.VMEM((slab_local * blks, 2, outer, 2 * half), bf16),
            pltpu.VMEM((row_count, 4, outer, half), f32),
            pltpu.VMEM((row_count, 2, 8, 2 * half), f32),
            pltpu.VMEM((pairs, 2 * PAIR * outer, 2 * half), f32),
            pltpu.SemaphoreType.DMA((pairs, sources)),
            pltpu.SemaphoreType.DMA((pairs, sources)),
            pltpu.SemaphoreType.DMA((blks,)),
            pltpu.SemaphoreType.DMA((blks,)),
            pltpu.SemaphoreType.DMA((blks,)),
            pltpu.SemaphoreType.DMA((blks,)),
        ],
        compiler_params=pltpu.CompilerParams(
            collective_id=0, has_side_effects=True, vmem_limit_bytes=56 * 1024 * 1024
        ),
    )(shifts, slab_index, shaped, response, *tables)
    return image.reshape(2, row_count, rows * 2 * half)


def solution(mesh):
    in_specs = (
        P(None, "blk", ("turn", "strip")),
        P(None, "blk", None),
        P(("blk", "turn")),
        P(("blk", "turn")),
    )
    out_specs = P(None, ("blk", "turn"), "strip")
    local = functools.partial(
        per_device, mesh.shape["turn"], mesh.shape["blk"], mesh.shape["strip"]
    )
    return jax.shard_map(local, mesh=mesh, in_specs=in_specs, out_specs=out_specs, check_vma=False)
```

profile of v0, /device:TPU:0, one launch (start us, length us, event | category | flops | bytes accessed | tf_op | source)
XLA Modules:
  0.0 44.4 jit_solution(8712818541391963706)
XLA Ops:
  0.0 0.0 copy-start
  0.0 1.2 %reshape.13 = bf16[2,2,128,2,128]{4,3,2,1,0:T(2,128)(2,1)S(1)} reshape(bf16[2,2,32768]{2,1,0:T(2,128)(2,1)} %param.9) | data formatting | bytes 524288 | tf_op jit(solution)/shard_map/reshape | solution.py:306
  1.2 0.3 copy.10
  1.6 0.9 %reshape.14.filt_ref = bf16[2,2,128,256]{3,2,1,0:T(8,128)(2,1)} reshape(bf16[2,2,128,2,128]{4,3,2,1,0:T(2,128)(2,1)S(1)} %bitcast.5) | data formatting | bytes 524288 | tf_op jit(solution)/shard_map/reshape | solution.py:308
  2.5 0.0 copy-done
  2.5 1.1 %copy.9 = bf16[64,2,4096]{2,1,0:T(2,128)(2,1)S(1)} copy(bf16[64,2,4096]{2,0,1:T(8,128)(2,1)S(1)} %bitcast.4) | data formatting | bytes 2097152 | tf_op jit(solution)/shard_map/transpose | solution.py:304
  3.6 1.5 %reshape.12.ech_ref = bf16[64,32,256]{2,1,0:T(8,128)(2,1)} reshape(bf16[64,2,4096]{2,1,0:T(2,128)(2,1)S(1)} %copy.9) | data formatting | bytes 2097152 | tf_op jit(solution)/shard_map/reshape | solution.py:304
  5.1 36.5 %shard_map.82 = f32[2,16,64,256]{3,2,1,0:T(8,128)} custom-call(s32[16]{0:T(128)} %shifts_ref.1, s32[16]{0:T(128)} %slabs_ref.1, bf16[64,32,256]{2,1,0:T(8,128)(2,1)} %reshape.12.ech_ref, bf16[2,2,128,256]{3,2,1,0:T(8,128)(2,1)} %reshape.14.filt_ref, bf16[2,512,256]{2,1,0:T(8,128)(2,1)} %constant.8.clone.one_ref, bf16[2,768,256]{2,1,0:T(8,128)(2,1)} %constant.9.clone.two_ref, ...), custom_call_target="tpu_custom_call" | custom-call | tf_op jit(solution)/shard_map/pallas_call | solution.py:313
  41.6 2.7 %reshape.15 = f32[2,16,16384]{2,1,0:T(8,128)} reshape(f32[2,16,64,256]{3,2,1,0:T(8,128)} %shard_map.82) | data formatting | bytes 4194304 | tf_op jit(solution)/shard_map/reshape | solution.py:335
Async XLA Ops:
  0.0 2.5 %copy-start = (bf16[2,64,4096]{2,1,0:T(8,128)(2,1)S(1)}, bf16[2,64,4096]{2,1,0:T(8,128)(2,1)}, u32[]{:S(2)}) copy-start(bf16[2,64,4096]{2,1,0:T(8,128)(2,1)} %param.8) | copy-start | bytes 3145732
where the time goes:
time: 44.5 us; the launch traced here: 44.4 us
  Pallas kernels  36.5 us (82%)
  local copies, waits for them, and re-layouts  7.79 us (18%)
    pallas_call x1, Pallas kernels, per_device(): pl.pallas_call(functools.partial(body, turns, blks, strips, length), out_...  36.5 us
    reshape x1, local copies, waits for them, and re-layouts, per_device(): return image.reshape(2, row_count, rows * 2 * half)  2.74 us
    reshape x2, local copies, waits for them, and re-layouts, per_device(): filters.reshape(2, slab_local, half, 2, outer).transpose(1, 0, 4, 3, 2)  1.56 us
    reshape x1, local copies, waits for them, and re-layouts, per_device(): shaped = echoes.transpose(1, 0, 2).reshape(-1, 2 * local, 2 * half)  1.49 us
    transpose x1, local copies, waits for them, and re-layouts, per_device(): shaped = echoes.transpose(1, 0, 2).reshape(-1, 2 * local, 2 * half)  1.09 us
    reshape x1, local copies, waits for them, and re-layouts, per_device(): response = filters.reshape(2, slab_local, half, 2, outer).transpose(1, 0,...  0.91 us

commit v1 on v0

--- a/solution.py
+++ b/solution.py
@@ -104,14 +104,14 @@
 
 def body(
     turns, blks, strips, length,
-    shifts_ref, slabs_ref, ech_ref, filt_ref, one_ref, two_ref, twist_ref, last_ref,
-    out_ref,
-    recv, filt_all, inv_twist, ramp, spec,
-    send_sem, recv_sem, fsend, frecv, gsend, grecv,
+    shifts_ref, slabs_ref, ech_ref, filt_ref, one_hbm, two_hbm, twist_hbm, last_hbm,
+    out_hbm,
+    recv, filt_all, inv_twist, ramp, spec, one_ref, two_ref, twist_ref, last_ref, out_ref,
+    send_sem, recv_sem, fsend, frecv, gsend, grecv, own_sem, out_sem, load_sem,
 ):
     turn, blk, strip = lax.axis_index("turn"), lax.axis_index("blk"), lax.axis_index("strip")
-    row_count = recv.shape[0]
-    pairs = row_count // PAIR
+    pairs = recv.shape[0]
+    row_count = pairs * PAIR
     slab_local = filt_ref.shape[0]
     core = lax.rem(turn, 2)
     partner = turn + 1 - 2 * core
@@ -120,6 +120,26 @@
     def peer(dt, ds):
         return (lax.rem(turn + dt, turns), blk, lax.rem(strip + ds, strips))
 
+    me = turn * strips + strip
+    twist_load = pltpu.make_async_copy(twist_hbm, twist_ref, load_sem.at[0])
+    one_load = pltpu.make_async_copy(one_hbm, one_ref, load_sem.at[1])
+    two_load = pltpu.make_async_copy(two_hbm, two_ref, load_sem.at[2])
+    last_load = pltpu.make_async_copy(last_hbm.at[strip], last_ref, load_sem.at[3])
+    filter_load = pltpu.make_async_copy(
+        filt_ref, filt_all.at[pl.ds(blk * slab_local, slab_local)], load_sem.at[4]
+    )
+
+    def own_copy(step):
+        return pltpu.make_async_copy(
+            ech_ref.at[:, pl.ds(turn * row_count + step * PAIR, PAIR)],
+            recv.at[step, me],
+            own_sem.at[step],
+        )
+
+    def out_copy(step):
+        group = step // (8 // PAIR)
+        return pltpu.make_async_copy(out_ref.at[:, group], out_hbm.at[:, group], out_sem.at[group])
+
     barrier = pltpu.get_barrier_semaphore()
     for dt, ds in peers:
         pl.semaphore_signal(barrier, inc=1, device_id=peer(dt, ds), device_id_type=MESH)
@@ -127,15 +147,18 @@
         pl.semaphore_signal(
             barrier, inc=1, device_id=(turn, lax.rem(blk + dz, blks), strip), device_id_type=MESH
         )
+    twist_load.start()
+    one_load.start()
+    two_load.start()
+    last_load.start()
+    filter_load.start()
     pl.semaphore_wait(barrier, len(peers) + blks - 1)
-
-    me = turn * strips + strip
 
     def echo_copy(step, dt, ds):
         to = peer(dt, ds)
         return pltpu.make_async_remote_copy(
-            src_ref=ech_ref.at[pl.ds(to[0] * row_count + step * PAIR, PAIR)],
-            dst_ref=recv.at[pl.ds(step * PAIR, PAIR), me],
+            src_ref=ech_ref.at[:, pl.ds(to[0] * row_count + step * PAIR, PAIR)],
+            dst_ref=recv.at[step, me],
             send_sem=send_sem.at[step, dt * strips + ds],
             recv_sem=recv_sem.at[step, dt * strips + ds],
             device_id=to,
@@ -170,12 +193,10 @@
     def start_step(step, carry):
         for dt, ds in peers:
             echo_copy(step, dt, ds).start()
+        own_copy(step).start()
         return carry
 
     lax.fori_loop(0, pairs, start_step, 0)
-
-    recv[:, me] = ech_ref[pl.ds(turn * row_count, row_count)]
-    filt_all[pl.ds(blk * slab_local, slab_local)] = filt_ref[...]
 
     half = LANES
     outer = length // (2 * half)
@@ -197,7 +218,10 @@
         ramp[row, 1] = -ui
         return carry
 
+    twist_load.wait()
     lax.fori_loop(0, row_count, prepare, 0)
+    one_load.wait()
+    two_load.wait()
 
     def lefts(blocks):
         highs, lows = [], []
@@ -211,7 +235,8 @@
     def forward(step, carry):
         for dt, ds in peers:
             echo_copy(step, dt, ds).wait_recv()
-        rows = [recv[step * PAIR + i].reshape(2 * outer, 2 * half) for i in range(PAIR)]
+        own_copy(step).wait()
+        rows = [recv[step, :, :, i].reshape(2 * outer, 2 * half) for i in range(PAIR)]
         parts = []
         for side in range(2):
             lanes = slice(side * half, (side + 1) * half)
@@ -233,9 +258,9 @@
             lanes = slice(e * half, (e + 1) * half)
             for i in range(PAIR):
                 row = step * PAIR + i
-                picked = filt_all[slabs_ref[row]].astype(f32)
+                picked = filt_all[slabs_ref[row], :, e].astype(f32)
                 ur, ui = ramp[row, 0][:1, lanes], ramp[row, 1][:1, lanes]
-                gr, gi = cmul(picked[0][:, lanes], picked[1][:, lanes], ur, ui)
+                gr, gi = cmul(picked[0], picked[1], ur, ui)
                 base = (e * PAIR + i) * outer
                 z = spec[step, base : base + outer]
                 blocks.append(cmul(z[:, :half], z[:, half:], gr, gi))
@@ -255,13 +280,13 @@
         rows = outer // strips
         for side, value in enumerate((lows, highs)):
             high, low = split(jnp.concatenate(value, 1))
-            left = last_ref[strip, side]
+            left = last_ref[side]
             res = dot(left, high)
             res = res[: 2 * rows] + res[2 * rows :] + dot(left[: 2 * rows], low)
             for i in range(PAIR):
-                row = step * PAIR + i
+                place = lax.rem(step, 8 // PAIR) * PAIR + i + 8 * side
                 for part in range(2):
-                    out_ref[part, row, :, side * half : (side + 1) * half] = res[
+                    out_ref[part, step // (8 // PAIR), pl.ds(place, rows, stride=16), :] = res[
                         part * rows : (part + 1) * rows, i * half : (i + 1) * half
                     ]
         return carry
@@ -278,8 +303,14 @@
         relay_copy(dz).start()
     for dz in range(1, blks):
         relay_copy(dz).wait_recv()
+    filter_load.wait()
+    last_load.wait()
     lax.fori_loop(0, early, inverse, 0)
-    lax.fori_loop(early, pairs, both, 0)
+    groups = row_count // 8
+    per_group = 8 // PAIR
+    for group in range(groups):
+        lax.fori_loop(max(early, group * per_group), max(early, (group + 1) * per_group), both, 0)
+        out_copy(group * per_group).start()
 
     def end_step(step, carry):
         for dt, ds in peers:
@@ -290,6 +321,8 @@
     for dz in range(1, blks):
         filter_copy(dz).wait_send()
         relay_copy(dz).wait_send()
+    for group in range(groups):
+        out_copy(group * per_group).wait()
 
 
 def per_device(turns, blks, strips, echoes, filters, slab_index, shifts):
@@ -301,37 +334,42 @@
     row_count = slab_index.shape[0]
     slab_local = filters.shape[1]
     pairs = row_count // PAIR
-    shaped = echoes.transpose(1, 0, 2).reshape(-1, 2 * local, 2 * half)
-    response = (
-        filters.reshape(2, slab_local, half, 2, outer)
-        .transpose(1, 0, 4, 3, 2)
-        .reshape(slab_local, 2, outer, 2 * half)
-    )
+    shaped = echoes.reshape(2, -1, local, 2 * half)
+    response = filters.reshape(2, slab_local, half, 2, outer).transpose(1, 0, 3, 4, 2)
     tables = [jnp.asarray(t) for t in make_tables(length, sources, strips)]
-    vmem, smem = pl.BlockSpec(memory_space=pltpu.VMEM), pl.BlockSpec(memory_space=pltpu.SMEM)
+    hbm, smem = pl.BlockSpec(memory_space=pl.ANY), pl.BlockSpec(memory_space=pltpu.SMEM)
     rows = outer // strips
     image = pl.pallas_call(
         functools.partial(body, turns, blks, strips, length),
-        out_shape=jax.ShapeDtypeStruct((2, row_count, rows, 2 * half), f32),
-        in_specs=[smem, smem] + [vmem] * 6,
-        out_specs=vmem,
+        out_shape=jax.ShapeDtypeStruct((2, row_count // 8, rows * 16, half), f32),
+        in_specs=[smem, smem] + [hbm] * 6,
+        out_specs=hbm,
         scratch_shapes=[
-            pltpu.VMEM((row_count, sources, 2 * local, 2 * half), bf16),
-            pltpu.VMEM((slab_local * blks, 2, outer, 2 * half), bf16),
+            pltpu.VMEM((pairs, sources, 2, PAIR, local, 2 * half), bf16),
+            pltpu.VMEM((slab_local * blks, 2, 2, outer, half), bf16),
             pltpu.VMEM((row_count, 4, outer, half), f32),
             pltpu.VMEM((row_count, 2, 8, 2 * half), f32),
             pltpu.VMEM((pairs, 2 * PAIR * outer, 2 * half), f32),
+            pltpu.VMEM(tables[0].shape, bf16),
+            pltpu.VMEM(tables[1].shape, bf16),
+            pltpu.VMEM(tables[2].shape, f32),
+            pltpu.VMEM(tables[3].shape[1:], bf16),
+            pltpu.VMEM((2, row_count // 8, rows * 16, half), f32),
             pltpu.SemaphoreType.DMA((pairs, sources)),
             pltpu.SemaphoreType.DMA((pairs, sources)),
             pltpu.SemaphoreType.DMA((blks,)),
             pltpu.SemaphoreType.DMA((blks,)),
             pltpu.SemaphoreType.DMA((blks,)),
             pltpu.SemaphoreType.DMA((blks,)),
+            pltpu.SemaphoreType.DMA((pairs,)),
+            pltpu.SemaphoreType.DMA((row_count // 8,)),
+            pltpu.SemaphoreType.DMA((5,)),
         ],
         compiler_params=pltpu.CompilerParams(
             collective_id=0, has_side_effects=True, vmem_limit_bytes=56 * 1024 * 1024
         ),
     )(shifts, slab_index, shaped, response, *tables)
+    image = image.reshape(2, row_count // 8, rows * 2, 8, half).transpose(0, 1, 3, 2, 4)
     return image.reshape(2, row_count, rows * 2 * half)
 
 

time: 44.5 us -> 43 us (0.966)
  Pallas kernels: 36.5 us -> 35.2 us
    unnamed x2, local copies, waits for them, and re-layouts: 0.01 us -> 5.5 us
    reshape x5 -> x2, local copies, waits for them, and re-layouts: 6.7 us -> 2.02 us  [per_device(): filters.reshape(2, slab_local, half, 2, outer).transpose(1, 0, 3, 4, 2)]
    pallas_call x1, Pallas kernels: 36.5 us -> 35.2 us  [per_device(): pl.pallas_call(functools.partial(body, turns, blks, strips, length), out_...]
    transpose x1 -> x0, local copies, waits for them, and re-layouts: 1.09 us -> none  [per_device(): shaped = echoes.transpose(1, 0, 2).reshape(-1, 2 * local, 2 * half)]
where the time goes in v1:
time: 43 us; the launch traced here: 42.8 us
  Pallas kernels  35.2 us (82%)
  local copies, waits for them, and re-layouts  7.52 us (17%)
    pallas_call x1, Pallas kernels, per_device(): pl.pallas_call(functools.partial(body, turns, blks, strips, length), out_...  35.2 us
    unnamed x2, local copies, waits for them, and re-layouts  5.5 us
    reshape x2, local copies, waits for them, and re-layouts, per_device(): filters.reshape(2, slab_local, half, 2, outer).transpose(1, 0, 3, 4, 2)  2.02 us

profile of v1, /device:TPU:0, one launch (start us, length us, event | category | flops | bytes accessed | tf_op | source)
XLA Modules:
  0.0 42.8 jit_solution(12644797039231839862)
XLA Ops:
  0.0 1.2 %reshape.13 = bf16[2,2,128,2,128]{4,3,2,1,0:T(2,128)(2,1)S(1)} reshape(bf16[2,2,32768]{2,1,0:T(2,128)(2,1)} %param.9) | data formatting | bytes 524288 | tf_op jit(solution)/shard_map/reshape | solution.py:338
  1.2 0.9 %copy.9 = bf16[2,2,128,2,128]{2,4,3,0,1:T(8,128)(2,1)} copy(bf16[2,2,128,2,128]{4,3,2,1,0:T(2,128)(2,1)S(1)} %reshape.13) | data formatting | bytes 524288 | tf_op jit(solution)/shard_map/reshape | solution.py:338
  2.0 2.4 %copy.10 = bf16[16,8,16,256]{3,2,1,0:T(8,128)(2,1)} copy(bf16[16,8,16,256]{3,1,2,0:T(8,128)(2,1)} %bitcast.13) | data formatting | bytes 2097152
  4.5 35.2 %shard_map.82 = f32[2,2,1024,128]{3,2,1,0:T(8,128)} custom-call(s32[16]{0:T(128)} %shifts_ref.1, s32[16]{0:T(128)} %slabs_ref.1, bf16[2,64,16,256]{3,2,1,0:T(8,128)(2,1)} %bitcast.11, bf16[2,2,2,128,128]{4,3,2,1,0:T(8,128)(2,1)} %bitcast.12, bf16[2,512,256]{2,1,0:T(8,128)(2,1)} %constant.8.clone.one_hbm, bf16[2,768,256]{2,1,0:T(8,128)(2,1)} %constant.9.clone.two_hbm, ...), custom_call_target="tpu_custom_call" | custom-call | tf_op jit(solution)/shard_map/pallas_call | solution.py:342
  39.7 3.0 %copy.12 = f32[2,16,16384]{2,1,0:T(8,128)} copy(f32[2,16,16384]{2,1,0:T(8,128)} %bitcast.10) | data formatting | bytes 4194304

commit v2 on v1

--- a/solution.py
+++ b/solution.py
@@ -105,14 +105,14 @@
 def body(
     turns, blks, strips, length,
     shifts_ref, slabs_ref, ech_ref, filt_ref, one_hbm, two_hbm, twist_hbm, last_hbm,
-    out_hbm,
-    recv, filt_all, inv_twist, ramp, spec, one_ref, two_ref, twist_ref, last_ref, out_ref,
-    send_sem, recv_sem, fsend, frecv, gsend, grecv, own_sem, out_sem, load_sem,
+    out_ref,
+    recv, filt_all, inv_twist, ramp, spec, one_ref, two_ref, twist_ref, last_ref, ech_raw, filt_raw, staged, outbox,
+    send_sem, recv_sem, fsend, frecv, gsend, grecv, load_sem,
 ):
     turn, blk, strip = lax.axis_index("turn"), lax.axis_index("blk"), lax.axis_index("strip")
     pairs = recv.shape[0]
     row_count = pairs * PAIR
-    slab_local = filt_ref.shape[0]
+    slab_local = filt_ref.shape[1] * LANES // length
     core = lax.rem(turn, 2)
     partner = turn + 1 - 2 * core
     peers = [(dt, ds) for dt in range(turns) for ds in range(strips) if (dt, ds) != (0, 0)]
@@ -125,20 +125,10 @@
     one_load = pltpu.make_async_copy(one_hbm, one_ref, load_sem.at[1])
     two_load = pltpu.make_async_copy(two_hbm, two_ref, load_sem.at[2])
     last_load = pltpu.make_async_copy(last_hbm.at[strip], last_ref, load_sem.at[3])
-    filter_load = pltpu.make_async_copy(
-        filt_ref, filt_all.at[pl.ds(blk * slab_local, slab_local)], load_sem.at[4]
-    )
-
-    def own_copy(step):
-        return pltpu.make_async_copy(
-            ech_ref.at[:, pl.ds(turn * row_count + step * PAIR, PAIR)],
-            recv.at[step, me],
-            own_sem.at[step],
-        )
-
-    def out_copy(step):
-        group = step // (8 // PAIR)
-        return pltpu.make_async_copy(out_ref.at[:, group], out_hbm.at[:, group], out_sem.at[group])
+    echo_load = pltpu.make_async_copy(ech_ref, ech_raw, load_sem.at[4])
+    filter_load = pltpu.make_async_copy(filt_ref, filt_raw, load_sem.at[5])
+    echo_load.start()
+    filter_load.start()
 
     barrier = pltpu.get_barrier_semaphore()
     for dt, ds in peers:
@@ -151,13 +141,12 @@
     one_load.start()
     two_load.start()
     last_load.start()
-    filter_load.start()
     pl.semaphore_wait(barrier, len(peers) + blks - 1)
 
     def echo_copy(step, dt, ds):
         to = peer(dt, ds)
         return pltpu.make_async_remote_copy(
-            src_ref=ech_ref.at[:, pl.ds(to[0] * row_count + step * PAIR, PAIR)],
+            src_ref=outbox.at[to[0], step],
             dst_ref=recv.at[step, me],
             send_sem=send_sem.at[step, dt * strips + ds],
             recv_sem=recv_sem.at[step, dt * strips + ds],
@@ -167,7 +156,7 @@
 
     def filter_copy(dz):
         return pltpu.make_async_remote_copy(
-            src_ref=filt_ref.at[:, core],
+            src_ref=filt_all.at[pl.ds(blk * slab_local, slab_local), core],
             dst_ref=filt_all.at[pl.ds(blk * slab_local, slab_local), core],
             send_sem=fsend.at[dz],
             recv_sem=frecv.at[dz],
@@ -187,19 +176,62 @@
             device_id_type=MESH,
         )
 
+    half = LANES
+    outer = length // (2 * half)
+    local = ech_raw.shape[2] // 2
+    groups = row_count // 8
+    per_group = 8 // PAIR
+
+    def arrange(group):
+        def fill(to, carry):
+            for part in range(2):
+                values = ech_raw[part, to * groups + group].astype(f32)
+                staged[part] = values.reshape(2 * local * 8, half)
+            for part in range(2):
+                for row in range(8):
+                    for side in range(2):
+                        value = staged[part, pl.ds(side * 8 + row, local, stride=16), :]
+                        outbox[
+                            to, group * per_group + row // PAIR, part, row % PAIR, :,
+                            side * half : (side + 1) * half,
+                        ] = value.astype(bf16)
+            return carry
+
+        lax.fori_loop(0, turns, fill, 0)
+        first, end = group * per_group, (group + 1) * per_group
+
+        def start_step(step, carry):
+            for dt, ds in peers:
+                echo_copy(step, dt, ds).start()
+            return carry
+
+        lax.fori_loop(first, end, start_step, 0)
+
+        def keep(step, carry):
+            recv[step, me] = outbox[turn, step]
+            return carry
+
+        lax.fori_loop(first, end, keep, 0)
+
+    echo_load.wait()
+    arrange(0)
+    filter_load.wait()
+    bins = filt_raw.shape[1]
+    bin_ids = lax.broadcasted_iota(jnp.int32, (bins, half), 0)
+    d_ids = lax.broadcasted_iota(jnp.int32, (bins, half), 1)
+    for s in range(slab_local):
+        for e in range(2):
+            picker = (bin_ids == (d_ids * 2 + e) * slab_local + s).astype(f32).astype(bf16)
+            for part in range(2):
+                got = lax.dot_general(
+                    filt_raw[part], picker, (((0,), (0,)), ((), ())), preferred_element_type=f32
+                )
+                filt_all[blk * slab_local + s, part, e] = got.astype(bf16)
     for dz in range(1, blks):
         filter_copy(dz).start()
-
-    def start_step(step, carry):
-        for dt, ds in peers:
-            echo_copy(step, dt, ds).start()
-        own_copy(step).start()
-        return carry
-
-    lax.fori_loop(0, pairs, start_step, 0)
-
-    half = LANES
-    outer = length // (2 * half)
+    for group in range(1, groups):
+        arrange(group)
+
     c_ids = lax.broadcasted_iota(jnp.int32, (outer, half), 0)
     lane_ids = lax.broadcasted_iota(jnp.int32, (8, 2 * half), 1)
     k_ids = jnp.where(lane_ids >= half, (lane_ids - half) * (2 * outer) + outer, lane_ids * (2 * outer))
@@ -235,7 +267,6 @@
     def forward(step, carry):
         for dt, ds in peers:
             echo_copy(step, dt, ds).wait_recv()
-        own_copy(step).wait()
         rows = [recv[step, :, :, i].reshape(2 * outer, 2 * half) for i in range(PAIR)]
         parts = []
         for side in range(2):
@@ -303,14 +334,9 @@
         relay_copy(dz).start()
     for dz in range(1, blks):
         relay_copy(dz).wait_recv()
-    filter_load.wait()
     last_load.wait()
     lax.fori_loop(0, early, inverse, 0)
-    groups = row_count // 8
-    per_group = 8 // PAIR
-    for group in range(groups):
-        lax.fori_loop(max(early, group * per_group), max(early, (group + 1) * per_group), both, 0)
-        out_copy(group * per_group).start()
+    lax.fori_loop(early, pairs, both, 0)
 
     def end_step(step, carry):
         for dt, ds in peers:
@@ -321,8 +347,6 @@
     for dz in range(1, blks):
         filter_copy(dz).wait_send()
         relay_copy(dz).wait_send()
-    for group in range(groups):
-        out_copy(group * per_group).wait()
 
 
 def per_device(turns, blks, strips, echoes, filters, slab_index, shifts):
@@ -334,16 +358,17 @@
     row_count = slab_index.shape[0]
     slab_local = filters.shape[1]
     pairs = row_count // PAIR
-    shaped = echoes.reshape(2, -1, local, 2 * half)
-    response = filters.reshape(2, slab_local, half, 2, outer).transpose(1, 0, 3, 4, 2)
+    shaped = echoes.reshape(2, -1, 8, 2 * local, half).transpose(0, 1, 3, 2, 4)
+    response = filters.reshape(2, slab_local, 2 * outer, half).transpose(0, 2, 1, 3)
+    response = response.reshape(2, -1, half)
     tables = [jnp.asarray(t) for t in make_tables(length, sources, strips)]
-    hbm, smem = pl.BlockSpec(memory_space=pl.ANY), pl.BlockSpec(memory_space=pltpu.SMEM)
+    hbm, smem = pl.BlockSpec(memory_space=pltpu.HBM), pl.BlockSpec(memory_space=pltpu.SMEM)
     rows = outer // strips
     image = pl.pallas_call(
         functools.partial(body, turns, blks, strips, length),
         out_shape=jax.ShapeDtypeStruct((2, row_count // 8, rows * 16, half), f32),
         in_specs=[smem, smem] + [hbm] * 6,
-        out_specs=hbm,
+        out_specs=pl.BlockSpec(memory_space=pltpu.VMEM),
         scratch_shapes=[
             pltpu.VMEM((pairs, sources, 2, PAIR, local, 2 * half), bf16),
             pltpu.VMEM((slab_local * blks, 2, 2, outer, half), bf16),
@@ -354,16 +379,17 @@
             pltpu.VMEM(tables[1].shape, bf16),
             pltpu.VMEM(tables[2].shape, f32),
             pltpu.VMEM(tables[3].shape[1:], bf16),
-            pltpu.VMEM((2, row_count // 8, rows * 16, half), f32),
+            pltpu.VMEM(shaped.shape, bf16),
+            pltpu.VMEM(response.shape, bf16),
+            pltpu.VMEM((2, 16 * local, half), f32),
+            pltpu.VMEM((turns, pairs, 2, PAIR, local, 2 * half), bf16),
             pltpu.SemaphoreType.DMA((pairs, sources)),
             pltpu.SemaphoreType.DMA((pairs, sources)),
             pltpu.SemaphoreType.DMA((blks,)),
             pltpu.SemaphoreType.DMA((blks,)),
             pltpu.SemaphoreType.DMA((blks,)),
             pltpu.SemaphoreType.DMA((blks,)),
-            pltpu.SemaphoreType.DMA((pairs,)),
-            pltpu.SemaphoreType.DMA((row_count // 8,)),
-            pltpu.SemaphoreType.DMA((5,)),
+            pltpu.SemaphoreType.DMA((6,)),
         ],
         compiler_params=pltpu.CompilerParams(
             collective_id=0, has_side_effects=True, vmem_limit_bytes=56 * 1024 * 1024

time: 43 us -> 39 us (0.907)
  local copies, waits for them, and re-layouts: 7.52 us -> 3.05 us
  Pallas kernels: 35.2 us -> 35.8 us
    unnamed x2 -> x1, local copies, waits for them, and re-layouts: 5.5 us -> 3.05 us
    reshape x2 -> x0, local copies, waits for them, and re-layouts: 2.02 us -> none  [per_device(): filters.reshape(2, slab_local, half, 2, outer).transpose(1, 0, 3, 4, 2)]
    pallas_call x1, Pallas kernels: 35.2 us -> 35.8 us  [per_device(): pl.pallas_call(functools.partial(body, turns, blks, strips, length), out_...]
where the time goes in v2:
time: 39 us; the launch traced here: 38.9 us
  Pallas kernels  35.8 us (92%)
  local copies, waits for them, and re-layouts  3.05 us (8%)
    pallas_call x1, Pallas kernels, per_device(): pl.pallas_call(functools.partial(body, turns, blks, strips, length), out_...  35.8 us
    unnamed x1, local copies, waits for them, and re-layouts  3.05 us

profile of v2, /device:TPU:0, one launch (start us, length us, event | category | flops | bytes accessed | tf_op | source)
XLA Modules:
  0.0 38.9 jit_solution(12800881185762003782)
XLA Ops:
  0.0 35.8 %shard_map.82 = f32[2,2,1024,128]{3,2,1,0:T(8,128)} custom-call(s32[16]{0:T(128)} %shifts_ref.1, s32[16]{0:T(128)} %slabs_ref.1, bf16[2,8,32,8,128]{4,3,2,1,0:T(8,128)(2,1)} %bitcast.14, bf16[2,512,128]{2,1,0:T(8,128)(2,1)} %bitcast.15, bf16[2,512,256]{2,1,0:T(8,128)(2,1)} %constant.8.clone.one_hbm, bf16[2,768,256]{2,1,0:T(8,128)(2,1)} %constant.9.clone.two_hbm, ...), custom_call_target="tpu_custom_call" | custom-call | tf_op jit(solution)/shard_map/pallas_call | solution.py:367
  35.8 3.0 %copy.11 = f32[2,16,16384]{2,1,0:T(8,128)} copy(f32[2,16,16384]{2,1,0:T(8,128)} %bitcast.13) | data formatting | bytes 4194304

commit v3 on v2

--- a/solution.py
+++ b/solution.py
@@ -327,7 +327,7 @@
         inverse(step, 0)
         return carry
 
-    early = pairs // 2
+    early = pairs * 5 // 8
     lax.fori_loop(0, early, forward, 0)
     for dz in range(1, blks):
         filter_copy(dz).wait_recv()

time: 39 us -> 41.2 us (1.056)
  Pallas kernels: 35.8 us -> 37.9 us
    pallas_call x1, Pallas kernels: 35.8 us -> 37.9 us  [per_device(): pl.pallas_call(functools.partial(body, turns, blks, strips, length), out_...]
where the time goes in v3:
time: 41.2 us; the launch traced here: 41 us
  Pallas kernels  37.9 us (92%)
  local copies, waits for them, and re-layouts  3.05 us (7%)
    pallas_call x1, Pallas kernels, per_device(): pl.pallas_call(functools.partial(body, turns, blks, strips, length), out_...  37.9 us
    unnamed x1, local copies, waits for them, and re-layouts  3.05 us

profile of v3, /device:TPU:0, one launch (start us, length us, event | category | flops | bytes accessed | tf_op | source)
XLA Modules:
  0.0 41.0 jit_solution(3224176030363543045)
XLA Ops:
  0.0 37.9 %shard_map.82 = f32[2,2,1024,128]{3,2,1,0:T(8,128)} custom-call(s32[16]{0:T(128)} %shifts_ref.1, s32[16]{0:T(128)} %slabs_ref.1, bf16[2,8,32,8,128]{4,3,2,1,0:T(8,128)(2,1)} %bitcast.14, bf16[2,512,128]{2,1,0:T(8,128)(2,1)} %bitcast.15, bf16[2,512,256]{2,1,0:T(8,128)(2,1)} %constant.8.clone.one_hbm, bf16[2,768,256]{2,1,0:T(8,128)(2,1)} %constant.9.clone.two_hbm, ...), custom_call_target="tpu_custom_call" | custom-call | tf_op jit(solution)/shard_map/pallas_call | solution.py:367
  38.0 3.0 %copy.11 = f32[2,16,16384]{2,1,0:T(8,128)} copy(f32[2,16,16384]{2,1,0:T(8,128)} %bitcast.13) | data formatting | bytes 4194304
